TPU v7x, 256 devices: a 4x2x16 block of a 4x16x16 slice. The times are simulated.
256 devices in a mesh: tracts: 2 (over y), sky: 32 (over z, core), depth: 4 (over x).
Axes of the slice: x: 4, y: 2, z: 16, core: 2. Of those that a mesh axis runs over, the one named last changes fastest.
The devices are a block of a 4x16x16 slice.
Arguments:
- visit_tiles: bfloat16 [1024, 32, 64, 512], P(('tracts', 'sky', 'depth')), parts along dimension 0, may hold values from -6 to 6
- warp_matrix: bfloat16 [1024, 512, 512], P(('tracts', 'sky', 'depth')), parts along dimension 0, may hold values from -0.25 to 0.25
- flux_scale: float32 [1024], P(('tracts', 'sky', 'depth')), parts along dimension 0, may hold values from 0.3 to 3
- patch_lists: int32 [1024, 32], P(('tracts', 'sky', 'depth')), parts along dimension 0, may hold values from 0 to 127, all different within a row; in each aligned block of 4 rows (0 to 3, 4 to 7, ...) at most 2 rows name the same one
- clip_bits: int32 [1024, 32, 4, 512], P(('tracts', 'sky', 'depth')), parts along dimension 0, may hold values from -2147483648 to 2147483647, as said below
Outputs:
- coadd_mean: float32 [2, 256, 64, 512], P(None, ('tracts', 'sky'), 'depth'), parts along dimension 1
- coadd_var: float32 [2, 256, 64, 512], P(None, ('tracts', 'sky'), 'depth'), parts along dimension 1
There are 2 independent parts, one for each index of `tracts`. A program takes and returns all parts, laid end to end along the dimension named above; each array names one. Nothing has to cross between parts.
Inputs may be any that keep to these rules, and one draw needn't show every extreme that they name: `patch_lists`: row v names the 32 different patches of visit v's blocks. In the rows of one device no patch is named more than 2 times, a bound that some block reaches there; every patch is named by some row. Bit 16 t + j of clip_bits[v, k, g, c] is 1 when clip pass t (t = 0 or 1) keeps the sample of visit v's block k at row 16 g + j, column c.
All inputs are finite; a program needn't handle non-finite values.
Results may differ from a plain program's by a relative error of at most 0.0029.
Values may be sent and summed in bfloat16 or wider, within the bound.
No kernel may reach another device: no remote copies, remote signals or barrier semaphores. Data moves between devices by JAX's collectives and lax.ppermute only.
A program may use at most 128 MiB of HBM per device.

v0:
```python
import jax
import jax.numpy as jnp
from jax import lax
from jax.sharding import PartitionSpec as P

PATCH_DEV = 4
CAPACITY = 2


def unpack_keep(packed, offset):
    positions = jnp.arange(16, dtype=jnp.int32) + offset
    bit_flags = jnp.bitwise_and(jnp.right_shift(packed[..., None, :], positions[:, None]), 1)
    target_shape = packed.shape[:-2] + (packed.shape[-2] * 16, packed.shape[-1])
    return bit_flags.reshape(target_shape).astype(jnp.float32)


def finish(count_first, sum_first, square_first, count_both, shift_sum, shift_square):
    first_mean = sum_first / jnp.maximum(count_first, 1.0)
    first_var = (square_first - sum_first * first_mean) / jnp.maximum(count_first - 1.0, 1.0)
    final_mean = first_mean + shift_sum / jnp.maximum(count_both, 1.0)
    final_var = (shift_square - shift_sum * shift_sum / jnp.maximum(count_both, 1.0)) / jnp.maximum(
        count_both - 1.0, 1.0
    )
    return (jnp.stack([first_mean, final_mean]), jnp.stack([first_var, final_var]))


def first_sums(samples, keep_first):
    count_first = jnp.sum(keep_first, axis=(0, 2))
    sum_first = jnp.sum(keep_first * samples, axis=(0, 2))
    square_first = jnp.sum(keep_first * samples * samples, axis=(0, 2))
    return (count_first, sum_first, square_first)


def stack_rows(pieces):
    received, packed = pieces
    samples = received.astype(jnp.float32)
    keep_first = unpack_keep(packed, 0)
    keep_both = keep_first * unpack_keep(packed, 16)
    count_first, sum_first, square_first = first_sums(samples, keep_first)
    first_mean = sum_first / jnp.maximum(count_first, 1.0)
    centred = samples - first_mean[None, :, None]
    count_both = jnp.sum(keep_both, axis=(0, 2))
    shift_sum = jnp.sum(keep_both * centred, axis=(0, 2))
    shift_square = jnp.sum(keep_both * centred * centred, axis=(0, 2))
    return finish(count_first, sum_first, square_first, count_both, shift_sum, shift_square)


def per_device(visit_tiles, warp_matrix, flux_scale, patch_lists, clip_bits):
    visits_here, intersections_here, block_rows, columns = visit_tiles.shape
    entries = visits_here * intersections_here
    sky_size = lax.axis_size("sky")
    depth_size = lax.axis_size("depth")
    patches = PATCH_DEV * sky_size
    warped = jnp.einsum(
        "vkrc,vcf->vkrf", visit_tiles, warp_matrix, preferred_element_type=jnp.float32
    )
    warped = (warped * flux_scale[:, None, None, None]).astype(jnp.bfloat16)
    targets = patch_lists.reshape(entries)
    onehot = (targets[:, None] == jnp.arange(patches, dtype=jnp.int32)[None, :]).astype(jnp.int32)
    earlier = jnp.cumsum(onehot, axis=0) - onehot
    slot_rank = jnp.sum(earlier * onehot, axis=1)
    source = jnp.full((patches * CAPACITY,), entries, jnp.int32)
    source = source.at[targets * CAPACITY + slot_rank].set(jnp.arange(entries, dtype=jnp.int32))
    rows_share = block_rows // depth_size
    depth_ids = jnp.arange(depth_size, dtype=jnp.int32)
    gather_index = (
        source.reshape(sky_size, 1, PATCH_DEV * CAPACITY) * depth_size + depth_ids[None, :, None]
    )
    send_tiles = jnp.take(
        warped.reshape(entries * depth_size, rows_share, columns),
        gather_index,
        axis=0,
        mode="fill",
        fill_value=0,
    )
    send_bits = jnp.take(
        clip_bits.reshape(entries * depth_size, rows_share // 16, columns),
        gather_index,
        axis=0,
        mode="fill",
        fill_value=0,
    )
    send_tiles = send_tiles.reshape(sky_size * depth_size, PATCH_DEV, CAPACITY, rows_share, columns)
    send_bits = send_bits.reshape(
        sky_size * depth_size, PATCH_DEV, CAPACITY, rows_share // 16, columns
    )
    mean_out, var_out = stack_rows(
        (
            lax.all_to_all(send_tiles, ("sky", "depth"), split_axis=0, concat_axis=0, tiled=True),
            lax.all_to_all(send_bits, ("sky", "depth"), split_axis=0, concat_axis=0, tiled=True),
        )
    )
    return (mean_out, var_out)


def solution(mesh):
    placed = (
        P(("tracts", "sky", "depth"), None, None, None),
        P(("tracts", "sky", "depth"), None, None),
        P(("tracts", "sky", "depth")),
        P(("tracts", "sky", "depth"), None),
        P(("tracts", "sky", "depth"), None, None, None),
    )
    return jax.shard_map(
        per_device,
        mesh=mesh,
        in_specs=placed,
        out_specs=(
            P(None, ("tracts", "sky"), "depth", None),
            P(None, ("tracts", "sky"), "depth", None),
        ),
        check_vma=False,
    )
```

profile of v0, /device:TPU:33, one launch (start us, length us, event | category | flops | bytes accessed | tf_op | source)
XLA Modules:
  0.0 913.9 jit_solution(7155397547654130632)
XLA Ops:
  0.6 0.0 copy-start
  0.6 0.9 eq.15
  1.6 0.7 broadcast_multiply_fusion
  2.2 0.1 fusion.9
  2.3 0.2 reduce_window_sum.11
  2.5 0.2 select_reduce_fusion
  2.7 0.1 mul.80
  2.8 1.0 scatter_custom_fusion
  3.8 0.1 mul.84
  3.9 0.1 copy.10
  4.0 0.1 reshape.225
  4.1 0.1 add.122
  4.2 0.1 add.123
  4.3 0.1 add.125
  4.4 0.2 copy.11
  4.6 0.0 copy-start.2
  4.6 1.6 reshape.221
  6.2 4.9 gather_fusion
  11.1 3.5 gather.13
  14.6 3.5 bitcast_select_fusion
  18.1 31.1 %all-to-all-start = ((s32[128,4,2,1,512]{4,2,1,3,0:T(2,128)}), s32[128,4,2,1,512]{4,2,1,3,0:T(2,128)}, u32[]{:S(2)}, u32[]{:S(2)}) async-start(s32[128,4,2,1,512]{4,2,1,3,0:T(2,128)} %bitcast_select_fusion), calls=%async_computation | async-start | bytes 4194304 | tf_op jit(solution)/shard_map/all_to_all | solution.py:90
  49.2 0.0 copy-done
  49.2 0.0 copy-done.2
  49.2 10.1 %multiply_convert_fusion = bf16[4,32,64,512]{3,2,1,0:T(8,128)(2,1)} fusion(bf16[4,32,64,512]{3,2,1,0:T(8,128)(2,1)} %param.5, f32[4]{0:T(128)S(1)} %copy-done.2, bf16[4,512,512]{2,1,0:T(8,128)(2,1)S(1)} %copy-done), kind=kOutput, calls=%fused_computation.16 | convolution fusion | flops 4303355904 | bytes 18874384 | tf_op jit(solution)/shard_map/vkrc,vcf->vkrf/dot_general | solution.py:54
  59.3 15.8 %gather_fusion.1 = bf16[1024,16,512]{2,1,0:T(8,128)(2,1)} fusion(bf16[512,16,512]{2,1,0:T(8,128)(2,1)} %bitcast.61, s32[1024]{0:T(1024)S(1)} %broadcast_clamp_fusion), kind=kCustom, calls=%fused_computation.1 | custom fusion | bytes 33558528 | tf_op jit(solution)/shard_map/jit(_take)/gather | solution.py:69
  75.1 14.0 %broadcast_select_fusion = bf16[128,4,2,16,512]{4,3,2,1,0:T(8,128)(2,1)} fusion(bf16[128,4,2,16,512]{4,3,2,1,0:T(8,128)(2,1)} %bitcast.60, pred[128,4,2]{2,1,0:T(4,128)(4,1)S(1)} %copy.11), kind=kLoop, calls=%fused_computation.17 | loop fusion | flops 8388608 | bytes 33555456 | tf_op jit(solution)/shard_map/jit(_take)/select_n | solution.py:69
  89.1 58.0 %all-to-all-done = s32[128,4,2,1,512]{4,2,1,3,0:T(2,128)} async-done(((s32[128,4,2,1,512]{4,2,1,3,0:T(2,128)}), s32[128,4,2,1,512]{4,2,1,3,0:T(2,128)}, u32[]{:S(2)}, u32[]{:S(2)}) %all-to-all-start) | async-done | bytes 2097184 | tf_op jit(solution)/shard_map/all_to_all | solution.py:90
  147.1 9.9 %all-to-all-start.1 = ((bf16[128,4,2,16,512]{4,3,2,1,0:T(8,128)(2,1)}), bf16[128,4,2,16,512]{4,3,2,1,0:T(8,128)(2,1)}, u32[]{:S(2)}, u32[]{:S(2)}) async-start(bf16[128,4,2,16,512]{4,3,2,1,0:T(8,128)(2,1)} %broadcast_select_fusion), calls=%async_computation.1 | async-start | bytes 33554432 | tf_op jit(solution)/shard_map/all_to_all | solution.py:89
  157.0 724.7 %all-to-all-done.1 = bf16[128,4,2,16,512]{4,3,2,1,0:T(8,128)(2,1)} async-done(((bf16[128,4,2,16,512]{4,3,2,1,0:T(8,128)(2,1)}), bf16[128,4,2,16,512]{4,3,2,1,0:T(8,128)(2,1)}, u32[]{:S(2)}, u32[]{:S(2)}) %all-to-all-start.1) | async-done | bytes 16777248 | tf_op jit(solution)/shard_map/all_to_all | solution.py:89
  881.7 0.0 copy-start.1
  881.7 10.6 %convert_reduce_fusion = (f32[4,16,512]{2,1,0:T(8,128)S(1)}, f32[4,16,512]{2,1,0:T(8,128)S(1)}) fusion(s32[128,4,2,512]{3,2,1,0:T(2,128)} %bitcast.3, bf16[128,4,2,16,512]{4,3,2,1,0:T(8,128)(2,1)} %all-to-all-done.1), kind=kLoop, calls=%fused_computation.11 | loop fusion | flops 58654720 | bytes 19136512 | tf_op jit(solution)/shard_map/reduce_sum | solution.py:28
  892.4 20.6 %fusion.2 = (f32[4,16,512]{2,1,0:T(8,128)S(1)}, f32[4,16,512]{2,1,0:T(8,128)S(1)}, f32[4,16,512]{2,1,0:T(8,128)S(1)}, f32[4,16,512]{2,1,0:T(8,128)S(1)}) fusion(bf16[128,4,2,16,512]{4,3,2,1,0:T(8,128)(2,1)} %all-to-all-done.1, f32[4,16,512]{2,1,0:T(8,128)S(1)} %maximum_divide_fusion, s32[16]{0:T(128)S(1)} %iota_add_fusion, s32[128,4,2,512]{3,2,1,0:T(2,128)} %bitcast.3), kind=kLoop, calls=%fused_computation.8 | loop fusion | flops 142475264 | bytes 19529792 | tf_op jit(solution)/shard_map/reduce_sum | solution.py:44
  913.0 0.1 bitcast_divide_fusion.1
  913.1 0.8 pad_maximum_fusion
  913.9 0.0 copy-done.1
  (9 shorter events, 0.1 us)
Async XLA Ops:
  0.6 48.6 %copy-start = (bf16[4,512,512]{2,1,0:T(8,128)(2,1)S(1)}, bf16[4,512,512]{2,1,0:T(8,128)(2,1)}, u32[]{:S(2)}) copy-start(bf16[4,512,512]{2,1,0:T(8,128)(2,1)} %param.6) | copy-start | bytes 6291460
  4.6 44.6 %copy-start.2 = (f32[4]{0:T(128)S(1)}, f32[4]{0:T(128)}, u32[]{:S(2)}) copy-start(f32[4]{0:T(128)} %param.7) | copy-start | bytes 52
  18.1 129.0 %all-to-all-start = ((s32[128,4,2,1,512]{4,2,1,3,0:T(2,128)}), s32[128,4,2,1,512]{4,2,1,3,0:T(2,128)}, u32[]{:S(2)}, u32[]{:S(2)}) async-start(s32[128,4,2,1,512]{4,2,1,3,0:T(2,128)} %bitcast_select_fusion), calls=%async_computation | async-start | bytes 4194304 | tf_op jit(solution)/shard_map/all_to_all | solution.py:90
  147.1 734.6 %all-to-all-start.1 = ((bf16[128,4,2,16,512]{4,3,2,1,0:T(8,128)(2,1)}), bf16[128,4,2,16,512]{4,3,2,1,0:T(8,128)(2,1)}, u32[]{:S(2)}, u32[]{:S(2)}) async-start(bf16[128,4,2,16,512]{4,3,2,1,0:T(8,128)(2,1)} %broadcast_select_fusion), calls=%async_computation.1 | async-start | bytes 33554432 | tf_op jit(solution)/shard_map/all_to_all | solution.py:89
  881.7 32.2 %copy-start.1 = (bf16[4,512,512]{2,1,0:T(8,128)(2,1)S(1)}, bf16[4,512,512]{2,1,0:T(8,128)(2,1)}, u32[]{:S(2)}) copy-start(bf16[4,512,512]{2,1,0:T(8,128)(2,1)} %param.6) | copy-start | bytes 6291460
where the time goes:
time: 914 us
  waiting for transfers between devices  783 us (86%)
  other arithmetic  50.9 us (6%)
  starting transfers between devices  40.9 us (4%)
  local copies, waits for them, and re-layouts  28.5 us (3%)
  matrix products  10.1 us (1%)
    all_to_all x1, waiting for transfers between devices, per_device(): lax.all_to_all(send_tiles, ('sky', 'depth'), split_axis=0, concat_axis=0,...  725 us
    all_to_all x1, waiting for transfers between devices, per_device(): lax.all_to_all(send_bits, ('sky', 'depth'), split_axis=0, concat_axis=0,...  58 us
    all_to_all x1, starting transfers between devices, per_device(): lax.all_to_all(send_bits, ('sky', 'depth'), split_axis=0, concat_axis=0,...  31.1 us
    reduce_sum x1, other arithmetic, stack_rows(): shift_square = jnp.sum(keep_both * centred * centred, axis=(0, 2))  20.6 us
  transfers between devices with their start and end apart: 2, of which 2 were waited for; matrix products, arithmetic and copies ran while one was open for 4% of the time, Pallas kernels for 0%

commit v1 on v0

v1 whole, which is shorter than its diff:
```python
import functools

import jax
import jax.numpy as jnp
from jax import lax
from jax.experimental import pallas as pl
from jax.experimental.pallas import tpu as pltpu
from jax.sharding import Mesh
from jax.sharding import PartitionSpec as P

PATCH_DEV = 4
CORES = 2
WORD_ROWS = 16
LANES = 128
GROUP = 4
WORDS = 8
SUMS = 5
RADIX = 4096


def warp_kernel(depth, part, half, where_ref, scale_ref, tiles_ref, matrix_ref, *out_refs):
    here, core = where_ref[0], where_ref[1]
    factor = scale_ref[pl.program_id(0)]
    blocks = tiles_ref.shape[1]
    sides = []
    for h in range(CORES):
        side = core if h == 0 else 1 - core
        start = pl.multiple_of(side * half + part * LANES, LANES)
        sides.append(matrix_ref[0, :, pl.ds(start, LANES)])
    matrix = jnp.concatenate(sides, axis=1)
    for k in range(depth):
        row = pl.multiple_of(lax.rem(here + k, depth) * WORD_ROWS, WORD_ROWS)
        rows = tiles_ref[0, :, pl.ds(row, WORD_ROWS), :].reshape(blocks * WORD_ROWS, -1)
        product = jnp.dot(rows, matrix, preferred_element_type=jnp.float32) * factor
        product = product.astype(jnp.bfloat16)
        for h in range(CORES):
            piece = product[:, h * LANES : (h + 1) * LANES]
            out_refs[k * CORES + h][...] = piece.reshape(blocks, WORD_ROWS, LANES)


def warp_part(visit_tiles, warp_matrix, flux_scale, where, depth, part):
    visits, blocks, rows, columns = visit_tiles.shape
    piece = jax.ShapeDtypeStruct((visits * blocks, WORD_ROWS, LANES), jnp.bfloat16)
    return pl.pallas_call(
        functools.partial(warp_kernel, depth, part, columns // CORES),
        out_shape=[piece] * (depth * CORES),
        grid=(visits,),
        in_specs=[
            pl.BlockSpec(memory_space=pltpu.SMEM),
            pl.BlockSpec(memory_space=pltpu.SMEM),
            pl.BlockSpec((1, blocks, rows, columns), lambda v: (v, 0, 0, 0)),
            pl.BlockSpec((1, columns, columns), lambda v: (v, 0, 0)),
        ],
        out_specs=[pl.BlockSpec((blocks, WORD_ROWS, LANES), lambda v: (v, 0, 0))] * (depth * CORES),
        name=f"warp_part{part}",
    )(where, flux_scale, visit_tiles, warp_matrix)


def sums_kernel(part, sources, patch_ref, *refs):
    tile_refs, bit_refs, out_ref = refs[:sources], refs[sources : 2 * sources], refs[-1]
    patches = out_ref.shape[0]
    entries = tile_refs[0].shape[0]
    positions = lax.broadcasted_iota(jnp.int32, (WORD_ROWS, LANES), 0)

    def clear(p, _):
        out_ref[p] = jnp.zeros(out_ref.shape[1:], jnp.float32)
        return 0

    lax.fori_loop(0, patches, clear, 0)
    for s in range(sources):

        def step(g, _, s=s):
            base = pl.multiple_of(g * WORDS, WORDS)
            words = bit_refs[s][pl.ds(base, WORDS), pl.ds(part * LANES, LANES)]
            for j in range(0, WORDS, GROUP):
                ids = [patch_ref[s, base + j + i] for i in range(GROUP)]
                held = [out_ref[p] for p in ids]
                for i in range(GROUP):
                    samples = tile_refs[s][base + j + i].astype(jnp.float32)
                    word = jnp.broadcast_to(words[j + i : j + i + 1], (WORD_ROWS, LANES))
                    kept = lax.bitwise_and(lax.shift_right_arithmetic(word, positions), 1)
                    both = lax.bitwise_and(
                        lax.shift_right_arithmetic(word, positions + WORD_ROWS), kept
                    )
                    counts = (kept + both * RADIX).astype(jnp.float32)
                    square = samples * samples
                    one, two = kept != 0, both != 0
                    out_ref[ids[i], 0] = held[i][0] + counts
                    out_ref[ids[i], 1] = held[i][1] + jnp.where(one, samples, 0.0)
                    out_ref[ids[i], 2] = held[i][2] + jnp.where(one, square, 0.0)
                    out_ref[ids[i], 3] = held[i][3] + jnp.where(two, samples, 0.0)
                    out_ref[ids[i], 4] = held[i][4] + jnp.where(two, square, 0.0)
            return 0

        lax.fori_loop(0, entries // WORDS, step, 0)


def sums_part(tiles, bits, patch_ids, patches, part):
    sources = len(tiles)
    return pl.pallas_call(
        functools.partial(sums_kernel, part, sources),
        out_shape=jax.ShapeDtypeStruct((patches, SUMS, WORD_ROWS, LANES), jnp.float32),
        in_specs=[pl.BlockSpec(memory_space=pltpu.SMEM)]
        + [pl.BlockSpec(memory_space=pltpu.VMEM)] * (2 * sources),
        out_specs=pl.BlockSpec(memory_space=pltpu.VMEM),
        name=f"sums_part{part}",
    )(patch_ids, *tiles, *bits)


def finish(sums):
    packed, sum_first, square_first, sum_both, square_both = (sums[:, i] for i in range(SUMS))
    count_both = jnp.floor(packed * (1.0 / RADIX))
    count_first = packed - count_both * RADIX
    first_mean = sum_first / jnp.maximum(count_first, 1.0)
    first_var = (square_first - sum_first * first_mean) / jnp.maximum(count_first - 1.0, 1.0)
    some = jnp.maximum(count_both, 1.0)
    shift_sum = sum_both - count_both * first_mean
    final_mean = first_mean + shift_sum / some
    final_var = (square_both - sum_both * (sum_both / some)) / jnp.maximum(count_both - 1.0, 1.0)
    return jnp.stack([first_mean, final_mean, first_var, final_var])


def per_device(visit_tiles, warp_matrix, flux_scale, patch_lists, clip_bits):
    visits, blocks, _, columns = visit_tiles.shape
    entries = visits * blocks
    chips, depth = lax.axis_size("chip"), lax.axis_size("depth")
    patches = PATCH_DEV * CORES * chips
    half = columns // CORES
    here, core = lax.axis_index("depth"), lax.axis_index("core")
    where = jnp.stack([here, core]).astype(jnp.int32)

    def place(d, c):
        return c * depth + d

    def send(value, k, h):
        if k == 0 and h == 0:
            return value
        pairs = [
            (place(d, c), place((d + k) % depth, c ^ h)) for c in range(CORES) for d in range(depth)
        ]
        return lax.ppermute(value, ("core", "depth"), pairs)

    words = clip_bits.reshape(entries, depth, CORES, half).transpose(1, 2, 0, 3)
    names = jnp.zeros((8, half), jnp.int32).at[0, :entries].set(patch_lists.reshape(entries))
    bits = []
    for k in range(depth):
        for h in range(CORES):
            message = words[lax.rem(here + k, depth), core if h == 0 else 1 - core]
            bits.append(send(jnp.concatenate([message, names]), k, h))
    patch_ids = jnp.stack([b[entries, :entries] for b in bits])

    parts = []
    for part in range(half // LANES):
        pieces = warp_part(visit_tiles, warp_matrix, flux_scale, where, depth, part)
        tiles = [send(pieces[k * CORES + h], k, h) for k in range(depth) for h in range(CORES)]
        sums = sums_part(tiles, bits, patch_ids, patches, part)
        parts.append(lax.psum_scatter(sums, "chip", scatter_dimension=0, tiled=True))
    results = finish(jnp.concatenate(parts, axis=-1))
    results = results.reshape(4, CORES, PATCH_DEV, WORD_ROWS, half)
    own, other = results[:, core], results[:, 1 - core]
    other = lax.ppermute(other, "core", [(c, c ^ 1) for c in range(CORES)])
    low, high = jnp.where(core == 0, own, other), jnp.where(core == 0, other, own)
    joined = jnp.concatenate([low, high], axis=-1)
    return joined[:2], joined[2:]


def solution(mesh):
    tracts, sky, depth = mesh.devices.shape
    fine = Mesh(
        mesh.devices.reshape(tracts, sky // CORES, CORES, depth),
        ("tracts", "chip", "core", "depth"),
    )
    every = ("tracts", "chip", "core", "depth")
    placed = (
        P(every, None, None, None),
        P(every, None, None),
        P(every),
        P(every, None),
        P(every, None, None, None),
    )
    out = P(None, ("tracts", "chip", "core"), "depth", None)
    return jax.shard_map(
        per_device, mesh=fine, in_specs=placed, out_specs=(out, out), check_vma=False
    )
```

time: 914 us -> 297 us (0.32)
  waiting for transfers between devices: 783 us -> 185 us
  other arithmetic: 50.9 us -> 2.39 us
  Pallas kernels: 0 us -> 39.5 us
  local copies, waits for them, and re-layouts: 28.5 us -> 5.31 us
  between operations: 0.81 us -> 14.4 us
  matrix products: 10.1 us -> 0 us
  starting transfers between devices: 40.9 us -> 50.1 us
    all_to_all x2 -> x0, waiting for transfers between devices: 783 us -> none  [the longest x1 725 us: per_device(): lax.all_to_all(send_tiles, ('sky', 'depth'), split_axis=0, concat_axis=0,...]
    ppermute x0 -> x22, waiting for transfers between devices: none -> 107 us  [the longest x21 106 us: send(): return lax.ppermute(value, ('core', 'depth'), pairs)]
    reduce_scatter x0 -> x2, waiting for transfers between devices: none -> 77.6 us  [per_device(): lax.psum_scatter(sums, 'chip', scatter_dimension=0, tiled=True)]
    ppermute x0 -> x22, starting transfers between devices: none -> 50 us  [the longest x21 39.8 us: send(): return lax.ppermute(value, ('core', 'depth'), pairs)]
    all_to_all x2 -> x0, starting transfers between devices: 40.9 us -> none  [the longest x1 31.1 us: per_device(): lax.all_to_all(send_bits, ('sky', 'depth'), split_axis=0, concat_axis=0,...]
    pallas_call x0 -> x4, Pallas kernels: none -> 39.5 us  [the longest x2 25.1 us: sums_part(): pl.pallas_call(functools.partial(sums_kernel, part, sources), out_shape=j...]
    reduce_sum x3 -> x0, other arithmetic: 31.4 us -> none  [the longest x1 20.6 us: stack_rows(): shift_square = jnp.sum(keep_both * centred * centred, axis=(0, 2))]
    gather x3 -> x0, local copies, waits for them, and re-layouts: 24.2 us -> none  [the longest x1 15.8 us: per_device(): jnp.take(warped.reshape(entries * depth_size, rows_share, columns), gathe...]
  transfers between devices with their start and end apart: 2 -> 24, of which waited for: 2 -> 16; matrix products, arithmetic and copies ran while one was open for 4% -> 1% of each run, Pallas kernels for 0% -> 7%
where the time goes in v1:
time: 297 us
  waiting for transfers between devices  185 us (62%)
  starting transfers between devices  50.1 us (17%)
  Pallas kernels  39.5 us (13%)
  between operations  14.4 us (5%)
  local copies, waits for them, and re-layouts  5.31 us (2%)
    ppermute x21, waiting for transfers between devices, send(): return lax.ppermute(value, ('core', 'depth'), pairs)  106 us
    reduce_scatter x2, waiting for transfers between devices, per_device(): lax.psum_scatter(sums, 'chip', scatter_dimension=0, tiled=True)  77.6 us
    ppermute x21, starting transfers between devices, send(): return lax.ppermute(value, ('core', 'depth'), pairs)  39.8 us
    pallas_call x2, Pallas kernels, sums_part(): pl.pallas_call(functools.partial(sums_kernel, part, sources), out_shape=j...  25.1 us
    pallas_call x2, Pallas kernels, warp_part(): pl.pallas_call(functools.partial(warp_kernel, depth, part, columns // COR...  14.3 us
    ppermute x1, starting transfers between devices, per_device(): other = lax.ppermute(other, 'core', [(c, c ^ 1) for c in range(CORES)])  10.1 us
  transfers between devices with their start and end apart: 24, of which 16 were waited for; matrix products, arithmetic and copies ran while one was open for 1% of the time, Pallas kernels for 7%

profile of v1, /device:TPU:33, one launch (start us, length us, event | category | flops | bytes accessed | tf_op | source)
XLA Modules:
  0.0 296.7 jit_solution(1349878075615081778)
XLA Ops:
  7.2 0.1 reduce-scatter.3.cloned.1.call-start
  7.2 0.6 pad_add_fusion.8.where_ref
  7.8 7.2 %warp_part0.1 = (bf16[128,16,128]{2,1,0:T(8,128)(2,1)}, bf16[128,16,128]{2,1,0:T(8,128)(2,1)}, bf16[128,16,128]{2,1,0:T(8,128)(2,1)}, bf16[128,16,128]{2,1,0:T(8...) custom-call(s32[2]{0:T(128)} %pad_add_fusion.8.where_ref, ...), custom_call_target="tpu_custom_call" | custom-call | tf_op jit(solution)/shard_map/warp_part0/pallas_call | solution.py:44
  15.0 20.5 %collective-permute-start.7 = (bf16[128,16,128]{2,1,0:T(8,128)(2,1)}, bf16[128,16,128]{2,1,0:T(8,128)(2,1)S(1)}, u32[]{:S(2)}, u32[]{:S(2)}) collective-permute-start(bf16[128,16,128]{2,1,0:T(8,128)(2,1)} %get-tuple-element.31), channel_id=1, source_target_pairs={{0,4},{1,5},{2,6},{3,7},{4,0},{5,1},{6,2},{7,3},{8,12},{9,13},{10,... | collective-permute-start | bytes 1572872 | tf_op jit(solution)/shard_map/ppermute | solution.py:141
  35.5 0.0 collective-permute-start.8
  35.5 0.1 slice.61
  35.6 0.9 reshape.222
  36.5 1.0 constant_dynamic-slice_fusion
  37.6 0.8 pad_add_fusion.7
  38.4 0.2 collective-permute-start
  38.6 0.0 collective-permute-start.1
  38.6 0.0 collective-permute-start.2
  38.6 1.2 collective-permute-done.refs_9_
  39.8 3.2 %collective-permute-start.3 = (s32[136,256]{1,0:T(8,128)S(1)}, s32[136,256]{1,0:T(8,128)S(1)}, u32[]{:S(2)}, u32[]{:S(2)}) collective-permute-start(s32[136,256]{1,0:T(8,128)S(1)} %get-tuple-element.71), channel_id=1, source_target_pairs={{0,2},{1,3},{2,0},{3,1},{4,6},{5,7},{6,4},{7,5},{8,10},{9,11},{10,... | collective-permute-start | bytes 417800 | tf_op jit(solution)/shard_map/ppermute | solution.py:141
  42.9 13.3 %collective-permute-done.1.refs_10_ = s32[136,256]{1,0:T(8,128)S(1)} collective-permute-done((s32[136,256]{1,0:T(8,128)S(1)}, s32[136,256]{1,0:T(8,128)S(1)}, u32[]{:S(2)}, u32[]{:S(2)}) %collective-permute-start.1) | collective-permute-done | bytes 139296 | tf_op jit(solution)/shard_map/ppermute | solution.py:141
  56.3 0.0 collective-permute-start.4
  56.3 3.3 %collective-permute-done.2.refs_11_ = s32[136,256]{1,0:T(8,128)S(1)} collective-permute-done((s32[136,256]{1,0:T(8,128)S(1)}, s32[136,256]{1,0:T(8,128)S(1)}, u32[]{:S(2)}, u32[]{:S(2)}) %collective-permute-start.2) | collective-permute-done | bytes 139296 | tf_op jit(solution)/shard_map/ppermute | solution.py:141
  59.6 0.0 collective-permute-start.5
  59.6 0.0 collective-permute-done.3.refs_12_
  59.6 0.5 collective-permute-start.6
  60.1 3.0 %collective-permute-done.4.refs_13_ = s32[136,256]{1,0:T(8,128)S(1)} collective-permute-done((s32[136,256]{1,0:T(8,128)S(1)}, s32[136,256]{1,0:T(8,128)S(1)}, u32[]{:S(2)}, u32[]{:S(2)}) %collective-permute-start.4) | collective-permute-done | bytes 139296 | tf_op jit(solution)/shard_map/ppermute | solution.py:141
  63.1 0.0 collective-permute-start.9
  63.1 1.6 collective-permute-done.5.refs_14_
  64.7 1.7 collective-permute-start.10
  66.4 1.5 collective-permute-done.6.refs_15_
  67.9 1.4 collective-permute-start.11
  69.3 0.0 collective-permute-done.7.refs_1_
  69.3 1.1 collective-permute-start.12
  70.4 0.0 collective-permute-done.8.refs_2_
  70.4 1.3 collective-permute-start.13
  71.8 0.6 stack.19.patch_ref
  72.4 28.5 %collective-permute-done.9.refs_3_ = bf16[128,16,128]{2,1,0:T(8,128)(2,1)S(1)} collective-permute-done((bf16[128,16,128]{2,1,0:T(8,128)(2,1)}, bf16[128,16,128]{2,1,0:T(8,128)(2,1)S(1)}, u32[]{:S(2)}, u32[]{:S(2)}) %collective-permute-start.9) | collective-permute-done | bytes 524320 | tf_op jit(solution)/shard_map/ppermute | solution.py:141
  100.9 0.0 collective-permute-done.10.refs_4_
  100.9 0.0 collective-permute-done.11.refs_5_
  100.9 1.2 collective-permute-done.12.refs_6_
  102.2 11.7 %collective-permute-done.13.refs_7_ = bf16[128,16,128]{2,1,0:T(8,128)(2,1)} collective-permute-done((bf16[128,16,128]{2,1,0:T(8,128)(2,1)}, bf16[128,16,128]{2,1,0:T(8,128)(2,1)}, u32[]{:S(2)}, u32[]{:S(2)}) %collective-permute-start.13) | collective-permute-done | bytes 524320 | tf_op jit(solution)/shard_map/ppermute | solution.py:141
  113.9 12.5 %sums_part0.1 = f32[128,5,16,128]{3,2,1,0:T(8,128)} custom-call(s32[8,128]{1,0:T(8,128)} %stack.19.patch_ref, bf16[128,16,128]{2,1,0:T(8,128)(2,1)} %get-tuple-element.30.refs_0_, bf16[128,16,128]{2,1,0:T(8,128)(2,1)} %copy-done.8, bf16[128,16,128]{2,1,0:T(8,128)(2,1)} %copy-done.9, bf16[128,16,128]{2,1,0:T(8,128)(2,1)} %copy-done.10, ...), custom_call_target="tpu_custom_call" | custom-call | tf_op jit(solution)/shard_map/sums_part0/pallas_call | solution.py:100
  126.4 0.1 reduce-scatter.3.cloned.1.call-update
  126.5 0.1 reduce-scatter.5.cloned.1.call-start
  126.6 7.2 %warp_part1.1 = (bf16[128,16,128]{2,1,0:T(8,128)(2,1)}, bf16[128,16,128]{2,1,0:T(8,128)(2,1)}, bf16[128,16,128]{2,1,0:T(8,128)(2,1)}, bf16[128,16,128]{2,1,0:T(8...) custom-call(s32[2]{0:T(128)} %pad_add_fusion.8.where_ref, ...), custom_call_target="tpu_custom_call" | custom-call | tf_op jit(solution)/shard_map/warp_part1/pallas_call | solution.py:44
  133.7 0.1 collective-permute-start.14
  133.9 0.6 collective-permute-start.15
  134.4 0.4 collective-permute-start.16
  134.8 3.6 %collective-permute-start.17 = (bf16[128,16,128]{2,1,0:T(8,128)(2,1)}, bf16[128,16,128]{2,1,0:T(8,128)(2,1)S(1)}, u32[]{:S(2)}, u32[]{:S(2)}) collective-permute-start(bf16[128,16,128]{2,1,0:T(8,128)(2,1)} %get-tuple-element.42), channel_id=1, source_target_pairs={{0,2},{1,3},{2,0},{3,1},{4,6},{5,7},{6,4},{7,5},{8,10},{9,11},{10,... | collective-permute-start | bytes 1572872 | tf_op jit(solution)/shard_map/ppermute | solution.py:141
  138.4 2.2 collective-permute-start.19
  140.6 8.3 %collective-permute-done.15.refs_2_ = bf16[128,16,128]{2,1,0:T(8,128)(2,1)S(1)} collective-permute-done((bf16[128,16,128]{2,1,0:T(8,128)(2,1)}, bf16[128,16,128]{2,1,0:T(8,128)(2,1)S(1)}, u32[]{:S(2)}, u32[]{:S(2)}) %collective-permute-start.15) | collective-permute-done | bytes 524320 | tf_op jit(solution)/shard_map/ppermute | solution.py:141
  148.9 3.0 %collective-permute-start.20 = (bf16[128,16,128]{2,1,0:T(8,128)(2,1)}, bf16[128,16,128]{2,1,0:T(8,128)(2,1)}, u32[]{:S(2)}, u32[]{:S(2)}) collective-permute-start(bf16[128,16,128]{2,1,0:T(8,128)(2,1)} %get-tuple-element.45), channel_id=1, source_target_pairs={{0,7},{1,4},{2,5},{3,6},{4,3},{5,0},{6,1},{7,2},{8,15},{9,12},{10,... | collective-permute-start | bytes 1572872 | tf_op jit(solution)/shard_map/ppermute | solution.py:141
  151.9 8.6 %collective-permute-done.16.refs_3_ = bf16[128,16,128]{2,1,0:T(8,128)(2,1)S(1)} collective-permute-done((bf16[128,16,128]{2,1,0:T(8,128)(2,1)}, bf16[128,16,128]{2,1,0:T(8,128)(2,1)S(1)}, u32[]{:S(2)}, u32[]{:S(2)}) %collective-permute-start.16) | collective-permute-done | bytes 524320 | tf_op jit(solution)/shard_map/ppermute | solution.py:141
  160.5 12.1 %collective-permute-done.17.refs_4_ = bf16[128,16,128]{2,1,0:T(8,128)(2,1)S(1)} collective-permute-done((bf16[128,16,128]{2,1,0:T(8,128)(2,1)}, bf16[128,16,128]{2,1,0:T(8,128)(2,1)S(1)}, u32[]{:S(2)}, u32[]{:S(2)}) %collective-permute-start.17) | collective-permute-done | bytes 524320 | tf_op jit(solution)/shard_map/ppermute | solution.py:141
  172.6 11.5 %collective-permute-done.18.refs_5_ = bf16[128,16,128]{2,1,0:T(8,128)(2,1)S(1)} collective-permute-done((bf16[128,16,128]{2,1,0:T(8,128)(2,1)}, bf16[128,16,128]{2,1,0:T(8,128)(2,1)S(1)}, u32[]{:S(2)}, u32[]{:S(2)}) %collective-permute-start.18) | collective-permute-done | bytes 524320 | tf_op jit(solution)/shard_map/ppermute | solution.py:141
  184.1 0.0 collective-permute-done.19.refs_6_
  184.1 0.4 collective-permute-done.20.refs_7_
  184.6 0.4 copy-done.16
  184.9 0.2 copy-done.17
  185.1 12.6 %sums_part1.1 = f32[128,5,16,128]{3,2,1,0:T(8,128)} custom-call(s32[8,128]{1,0:T(8,128)} %stack.19.patch_ref, bf16[128,16,128]{2,1,0:T(8,128)(2,1)} %get-tuple-element.38.refs_0_, bf16[128,16,128]{2,1,0:T(8,128)(2,1)} %copy-done.12, bf16[128,16,128]{2,1,0:T(8,128)(2,1)} %copy-done.13, bf16[128,16,128]{2,1,0:T(8,128)(2,1)} %copy-done.14, ...), custom_call_target="tpu_custom_call" | custom-call | tf_op jit(solution)/shard_map/sums_part1/pallas_call | solution.py:100
  197.7 0.1 reduce-scatter.5.cloned.1.call-update
  197.8 0.0 reduce-scatter.3.cloned.1.call-done
  197.8 1.0 constant_dynamic-update-slice_fusion.1
  198.8 77.5 %reduce-scatter.5.cloned.1.call-done = f32[8,5,16,128]{3,2,1,0:T(8,128)} async-done(((f32[128,5,16,128]{3,2,1,0:T(8,128)}), f32[8,5,16,128]{3,2,1,0:T(8,128)}) %reduce-scatter.5.cloned.1.call-update) | async-done | bytes 327696 | tf_op jit(solution)/shard_map/reduce_scatter | solution.py:157
  276.3 1.0 constant_dynamic-update-slice_fusion
  277.4 0.1 maximum_divide_fusion.1
  277.6 10.1 %collective-permute-start.21 = (f32[4,4,16,256]{3,2,1,0:T(8,128)S(1)}, f32[4,4,16,256]{3,2,1,0:T(8,128)S(1)}, u32[]{:S(2)}, u32[]{:S(2)}) collective-permute-start(f32[4,4,16,256]{3,2,1,0:T(8,128)S(1)} %dynamic-slice_bitcast_fusion), channel_id=1, source_target_pairs={{0,4},{4,0},{1,5},{5,1},{2,6},{6,2},{3,7},{7,3},{8,12},{12,8},{9,1... | collective-permute-start | bytes 786440 | tf_op jit(solution)/shard_map/ppermute | solution.py:161
  287.8 1.2 collective-permute-done.21
  289.0 0.9 pad_maximum_fusion.1
  (53 shorter events, 0.3 us)
Async XLA Ops:
  7.2 190.6 %reduce-scatter.3.cloned.1.call-start = ((), (), s32[]{:S(2)}) async-start(), calls=%async_computation.2 | async-start | bytes 5570560 | tf_op jit(solution)/shard_map/reduce_scatter | solution.py:157
  7.8 27.7 %copy-start.18 = (s32[4,32]{1,0:T(4,128)S(1)}, s32[4,32]{1,0:T(4,128)}, u32[]{:S(2)}) copy-start(s32[4,32]{1,0:T(4,128)} %param.10) | copy-start | bytes 1540
  7.8 27.8 %copy-start = (s32[4,32,4,512]{3,2,1,0:T(4,128)S(1)}, s32[4,32,4,512]{3,2,1,0:T(4,128)}, u32[]{:S(2)}) copy-start(s32[4,32,4,512]{3,2,1,0:T(4,128)} %param.11) | copy-start | bytes 3145732
  15.0 54.3 %collective-permute-start.7 = (bf16[128,16,128]{2,1,0:T(8,128)(2,1)}, bf16[128,16,128]{2,1,0:T(8,128)(2,1)S(1)}, u32[]{:S(2)}, u32[]{:S(2)}) collective-permute-start(bf16[128,16,128]{2,1,0:T(8,128)(2,1)} %get-tuple-element.31), channel_id=1, source_target_pairs={{0,4},{1,5},{2,6},{3,7},{4,0},{5,1},{6,2},{7,3},{8,12},{9,13},{10,... | collective-permute-start | bytes 1572872 | tf_op jit(solution)/shard_map/ppermute | solution.py:141
  35.5 34.9 %collective-permute-start.8 = (bf16[128,16,128]{2,1,0:T(8,128)(2,1)}, bf16[128,16,128]{2,1,0:T(8,128)(2,1)S(1)}, u32[]{:S(2)}, u32[]{:S(2)}) collective-permute-start(bf16[128,16,128]{2,1,0:T(8,128)(2,1)} %get-tuple-element.32), channel_id=1, source_target_pairs={{0,1},{1,2},{2,3},{3,0},{4,5},{5,6},{6,7},{7,4},{8,9},{9,10},{10,1... | collective-permute-start | bytes 1572872 | tf_op jit(solution)/shard_map/ppermute | solution.py:141
  38.4 1.4 collective-permute-start
  38.6 17.7 %collective-permute-start.1 = (s32[136,256]{1,0:T(8,128)S(1)}, s32[136,256]{1,0:T(8,128)S(1)}, u32[]{:S(2)}, u32[]{:S(2)}) collective-permute-start(s32[136,256]{1,0:T(8,128)S(1)} %get-tuple-element.69), channel_id=1, source_target_pairs={{0,1},{1,2},{2,3},{3,0},{4,5},{5,6},{6,7},{7,4},{8,9},{9,10},{10,1... | collective-permute-start | bytes 417800 | tf_op jit(solution)/shard_map/ppermute | solution.py:141
  38.6 21.0 %collective-permute-start.2 = (s32[136,256]{1,0:T(8,128)S(1)}, s32[136,256]{1,0:T(8,128)S(1)}, u32[]{:S(2)}, u32[]{:S(2)}) collective-permute-start(s32[136,256]{1,0:T(8,128)S(1)} %get-tuple-element.70), channel_id=1, source_target_pairs={{0,5},{1,6},{2,7},{3,4},{4,1},{5,2},{6,3},{7,0},{8,13},{9,14},{10,... | collective-permute-start | bytes 417800 | tf_op jit(solution)/shard_map/ppermute | solution.py:141
  39.8 74.1 %copy-start.1 = (s32[136,256]{1,0:T(8,128)}, s32[136,256]{1,0:T(8,128)S(1)}, u32[]{:S(2)}) copy-start(s32[136,256]{1,0:T(8,128)S(1)} %collective-permute-done.refs_9_) | copy-start | bytes 417796
  39.8 19.8 %collective-permute-start.3 = (s32[136,256]{1,0:T(8,128)S(1)}, s32[136,256]{1,0:T(8,128)S(1)}, u32[]{:S(2)}, u32[]{:S(2)}) collective-permute-start(s32[136,256]{1,0:T(8,128)S(1)} %get-tuple-element.71), channel_id=1, source_target_pairs={{0,2},{1,3},{2,0},{3,1},{4,6},{5,7},{6,4},{7,5},{8,10},{9,11},{10,... | collective-permute-start | bytes 417800 | tf_op jit(solution)/shard_map/ppermute | solution.py:141
  56.3 57.6 %copy-start.2 = (s32[136,256]{1,0:T(8,128)}, s32[136,256]{1,0:T(8,128)S(1)}, u32[]{:S(2)}) copy-start(s32[136,256]{1,0:T(8,128)S(1)} %collective-permute-done.1.refs_10_) | copy-start | bytes 417796
  56.3 6.9 %collective-permute-start.4 = (s32[136,256]{1,0:T(8,128)S(1)}, s32[136,256]{1,0:T(8,128)S(1)}, u32[]{:S(2)}, u32[]{:S(2)}) collective-permute-start(s32[136,256]{1,0:T(8,128)S(1)} %get-tuple-element.72), channel_id=1, source_target_pairs={{0,6},{1,7},{2,4},{3,5},{4,2},{5,3},{6,0},{7,1},{8,14},{9,15},{10,... | collective-permute-start | bytes 417800 | tf_op jit(solution)/shard_map/ppermute | solution.py:141
  59.6 54.3 %copy-start.3 = (s32[136,256]{1,0:T(8,128)}, s32[136,256]{1,0:T(8,128)S(1)}, u32[]{:S(2)}) copy-start(s32[136,256]{1,0:T(8,128)S(1)} %collective-permute-done.2.refs_11_) | copy-start | bytes 417796
  59.6 5.1 %collective-permute-start.5 = (s32[136,256]{1,0:T(8,128)S(1)}, s32[136,256]{1,0:T(8,128)S(1)}, u32[]{:S(2)}, u32[]{:S(2)}) collective-permute-start(s32[136,256]{1,0:T(8,128)S(1)} %get-tuple-element.73), channel_id=1, source_target_pairs={{0,3},{1,0},{2,1},{3,2},{4,7},{5,4},{6,5},{7,6},{8,11},{9,8},{10,9... | collective-permute-start | bytes 417800 | tf_op jit(solution)/shard_map/ppermute | solution.py:141
  59.6 54.3 %copy-start.4 = (s32[136,256]{1,0:T(8,128)}, s32[136,256]{1,0:T(8,128)S(1)}, u32[]{:S(2)}) copy-start(s32[136,256]{1,0:T(8,128)S(1)} %collective-permute-done.3.refs_12_) | copy-start | bytes 417796
  59.6 8.4 %collective-permute-start.6 = (s32[136,256]{1,0:T(8,128)S(1)}, s32[136,256]{1,0:T(8,128)S(1)}, u32[]{:S(2)}, u32[]{:S(2)}) collective-permute-start(s32[136,256]{1,0:T(8,128)S(1)} %get-tuple-element.74), channel_id=1, source_target_pairs={{0,7},{1,4},{2,5},{3,6},{4,3},{5,0},{6,1},{7,2},{8,15},{9,12},{10,... | collective-permute-start | bytes 417800 | tf_op jit(solution)/shard_map/ppermute | solution.py:141
  63.1 50.7 %copy-start.5 = (s32[136,256]{1,0:T(8,128)}, s32[136,256]{1,0:T(8,128)S(1)}, u32[]{:S(2)}) copy-start(s32[136,256]{1,0:T(8,128)S(1)} %collective-permute-done.4.refs_13_) | copy-start | bytes 417796
  63.1 37.8 %collective-permute-start.9 = (bf16[128,16,128]{2,1,0:T(8,128)(2,1)}, bf16[128,16,128]{2,1,0:T(8,128)(2,1)S(1)}, u32[]{:S(2)}, u32[]{:S(2)}) collective-permute-start(bf16[128,16,128]{2,1,0:T(8,128)(2,1)} %get-tuple-element.33), channel_id=1, source_target_pairs={{0,5},{1,6},{2,7},{3,4},{4,1},{5,2},{6,3},{7,0},{8,13},{9,14},{10,... | collective-permute-start | bytes 1572872 | tf_op jit(solution)/shard_map/ppermute | solution.py:141
  64.7 49.2 %copy-start.6 = (s32[136,256]{1,0:T(8,128)}, s32[136,256]{1,0:T(8,128)S(1)}, u32[]{:S(2)}) copy-start(s32[136,256]{1,0:T(8,128)S(1)} %collective-permute-done.5.refs_14_) | copy-start | bytes 417796
  64.7 36.2 %collective-permute-start.10 = (bf16[128,16,128]{2,1,0:T(8,128)(2,1)}, bf16[128,16,128]{2,1,0:T(8,128)(2,1)S(1)}, u32[]{:S(2)}, u32[]{:S(2)}) collective-permute-start(bf16[128,16,128]{2,1,0:T(8,128)(2,1)} %get-tuple-element.34), channel_id=1, source_target_pairs={{0,2},{1,3},{2,0},{3,1},{4,6},{5,7},{6,4},{7,5},{8,10},{9,11},{10,... | collective-permute-start | bytes 1572872 | tf_op jit(solution)/shard_map/ppermute | solution.py:141
  67.9 45.9 %copy-start.7 = (s32[136,256]{1,0:T(8,128)}, s32[136,256]{1,0:T(8,128)S(1)}, u32[]{:S(2)}) copy-start(s32[136,256]{1,0:T(8,128)S(1)} %collective-permute-done.6.refs_15_) | copy-start | bytes 417796
  67.9 33.0 %collective-permute-start.11 = (bf16[128,16,128]{2,1,0:T(8,128)(2,1)}, bf16[128,16,128]{2,1,0:T(8,128)(2,1)}, u32[]{:S(2)}, u32[]{:S(2)}) collective-permute-start(bf16[128,16,128]{2,1,0:T(8,128)(2,1)} %get-tuple-element.35), channel_id=1, source_target_pairs={{0,6},{1,7},{2,4},{3,5},{4,2},{5,3},{6,0},{7,1},{8,14},{9,15},{10,... | collective-permute-start | bytes 1572872 | tf_op jit(solution)/shard_map/ppermute | solution.py:141
  69.3 44.5 %copy-start.8 = (bf16[128,16,128]{2,1,0:T(8,128)(2,1)}, bf16[128,16,128]{2,1,0:T(8,128)(2,1)S(1)}, u32[]{:S(2)}) copy-start(bf16[128,16,128]{2,1,0:T(8,128)(2,1)S(1)} %collective-permute-done.7.refs_1_) | copy-start | bytes 1572868
  69.3 32.8 %collective-permute-start.12 = (bf16[128,16,128]{2,1,0:T(8,128)(2,1)}, bf16[128,16,128]{2,1,0:T(8,128)(2,1)}, u32[]{:S(2)}, u32[]{:S(2)}) collective-permute-start(bf16[128,16,128]{2,1,0:T(8,128)(2,1)} %get-tuple-element.36), channel_id=1, source_target_pairs={{0,3},{1,0},{2,1},{3,2},{4,7},{5,4},{6,5},{7,6},{8,11},{9,8},{10,9... | collective-permute-start | bytes 1572872 | tf_op jit(solution)/shard_map/ppermute | solution.py:141
  70.4 43.5 %copy-start.9 = (bf16[128,16,128]{2,1,0:T(8,128)(2,1)}, bf16[128,16,128]{2,1,0:T(8,128)(2,1)S(1)}, u32[]{:S(2)}) copy-start(bf16[128,16,128]{2,1,0:T(8,128)(2,1)S(1)} %collective-permute-done.8.refs_2_) | copy-start | bytes 1572868
  70.4 43.4 %collective-permute-start.13 = (bf16[128,16,128]{2,1,0:T(8,128)(2,1)}, bf16[128,16,128]{2,1,0:T(8,128)(2,1)}, u32[]{:S(2)}, u32[]{:S(2)}) collective-permute-start(bf16[128,16,128]{2,1,0:T(8,128)(2,1)} %get-tuple-element.37), channel_id=1, source_target_pairs={{0,7},{1,4},{2,5},{3,6},{4,3},{5,0},{6,1},{7,2},{8,15},{9,12},{10,... | collective-permute-start | bytes 1572872 | tf_op jit(solution)/shard_map/ppermute | solution.py:141
  100.9 13.0 %copy-start.10 = (bf16[128,16,128]{2,1,0:T(8,128)(2,1)}, bf16[128,16,128]{2,1,0:T(8,128)(2,1)S(1)}, u32[]{:S(2)}) copy-start(bf16[128,16,128]{2,1,0:T(8,128)(2,1)S(1)} %collective-permute-done.9.refs_3_) | copy-start | bytes 1572868
  100.9 13.0 %copy-start.11 = (bf16[128,16,128]{2,1,0:T(8,128)(2,1)}, bf16[128,16,128]{2,1,0:T(8,128)(2,1)S(1)}, u32[]{:S(2)}) copy-start(bf16[128,16,128]{2,1,0:T(8,128)(2,1)S(1)} %collective-permute-done.10.refs_4_) | copy-start | bytes 1572868
  126.5 149.9 %reduce-scatter.5.cloned.1.call-start = ((), (), s32[]{:S(2)}) async-start(), calls=%async_computation.3 | async-start | bytes 5570560 | tf_op jit(solution)/shard_map/reduce_scatter | solution.py:157
  133.7 4.7 %collective-permute-start.14 = (bf16[128,16,128]{2,1,0:T(8,128)(2,1)}, bf16[128,16,128]{2,1,0:T(8,128)(2,1)S(1)}, u32[]{:S(2)}, u32[]{:S(2)}) collective-permute-start(bf16[128,16,128]{2,1,0:T(8,128)(2,1)} %get-tuple-element.39), channel_id=1, source_target_pairs={{0,4},{1,5},{2,6},{3,7},{4,0},{5,1},{6,2},{7,3},{8,12},{9,13},{10,... | collective-permute-start | bytes 1572872 | tf_op jit(solution)/shard_map/ppermute | solution.py:141
  133.9 15.0 %collective-permute-start.15 = (bf16[128,16,128]{2,1,0:T(8,128)(2,1)}, bf16[128,16,128]{2,1,0:T(8,128)(2,1)S(1)}, u32[]{:S(2)}, u32[]{:S(2)}) collective-permute-start(bf16[128,16,128]{2,1,0:T(8,128)(2,1)} %get-tuple-element.40), channel_id=1, source_target_pairs={{0,1},{1,2},{2,3},{3,0},{4,5},{5,6},{6,7},{7,4},{8,9},{9,10},{10,1... | collective-permute-start | bytes 1572872 | tf_op jit(solution)/shard_map/ppermute | solution.py:141
  134.4 26.1 %collective-permute-start.16 = (bf16[128,16,128]{2,1,0:T(8,128)(2,1)}, bf16[128,16,128]{2,1,0:T(8,128)(2,1)S(1)}, u32[]{:S(2)}, u32[]{:S(2)}) collective-permute-start(bf16[128,16,128]{2,1,0:T(8,128)(2,1)} %get-tuple-element.41), channel_id=1, source_target_pairs={{0,5},{1,6},{2,7},{3,4},{4,1},{5,2},{6,3},{7,0},{8,13},{9,14},{10,... | collective-permute-start | bytes 1572872 | tf_op jit(solution)/shard_map/ppermute | solution.py:141
  134.8 37.8 %collective-permute-start.17 = (bf16[128,16,128]{2,1,0:T(8,128)(2,1)}, bf16[128,16,128]{2,1,0:T(8,128)(2,1)S(1)}, u32[]{:S(2)}, u32[]{:S(2)}) collective-permute-start(bf16[128,16,128]{2,1,0:T(8,128)(2,1)} %get-tuple-element.42), channel_id=1, source_target_pairs={{0,2},{1,3},{2,0},{3,1},{4,6},{5,7},{6,4},{7,5},{8,10},{9,11},{10,... | collective-permute-start | bytes 1572872 | tf_op jit(solution)/shard_map/ppermute | solution.py:141
  138.4 45.8 %collective-permute-start.18 = (bf16[128,16,128]{2,1,0:T(8,128)(2,1)}, bf16[128,16,128]{2,1,0:T(8,128)(2,1)S(1)}, u32[]{:S(2)}, u32[]{:S(2)}) collective-permute-start(bf16[128,16,128]{2,1,0:T(8,128)(2,1)} %get-tuple-element.43), channel_id=1, source_target_pairs={{0,6},{1,7},{2,4},{3,5},{4,2},{5,3},{6,0},{7,1},{8,14},{9,15},{10,... | collective-permute-start | bytes 1572872 | tf_op jit(solution)/shard_map/ppermute | solution.py:141
  138.4 46.2 %copy-start.12 = (bf16[128,16,128]{2,1,0:T(8,128)(2,1)}, bf16[128,16,128]{2,1,0:T(8,128)(2,1)S(1)}, u32[]{:S(2)}) copy-start(bf16[128,16,128]{2,1,0:T(8,128)(2,1)S(1)} %collective-permute-done.14.refs_1_) | copy-start | bytes 1572868
  138.4 45.7 %collective-permute-start.19 = (bf16[128,16,128]{2,1,0:T(8,128)(2,1)}, bf16[128,16,128]{2,1,0:T(8,128)(2,1)S(1)}, u32[]{:S(2)}, u32[]{:S(2)}) collective-permute-start(bf16[128,16,128]{2,1,0:T(8,128)(2,1)} %get-tuple-element.44), channel_id=1, source_target_pairs={{0,3},{1,0},{2,1},{3,2},{4,7},{5,4},{6,5},{7,6},{8,11},{9,8},{10,9... | collective-permute-start | bytes 1572872 | tf_op jit(solution)/shard_map/ppermute | solution.py:141
  148.9 35.7 %copy-start.13 = (bf16[128,16,128]{2,1,0:T(8,128)(2,1)}, bf16[128,16,128]{2,1,0:T(8,128)(2,1)S(1)}, u32[]{:S(2)}) copy-start(bf16[128,16,128]{2,1,0:T(8,128)(2,1)S(1)} %collective-permute-done.15.refs_2_) | copy-start | bytes 1572868
  148.9 35.7 %collective-permute-start.20 = (bf16[128,16,128]{2,1,0:T(8,128)(2,1)}, bf16[128,16,128]{2,1,0:T(8,128)(2,1)}, u32[]{:S(2)}, u32[]{:S(2)}) collective-permute-start(bf16[128,16,128]{2,1,0:T(8,128)(2,1)} %get-tuple-element.45), channel_id=1, source_target_pairs={{0,7},{1,4},{2,5},{3,6},{4,3},{5,0},{6,1},{7,2},{8,15},{9,12},{10,... | collective-permute-start | bytes 1572872 | tf_op jit(solution)/shard_map/ppermute | solution.py:141
  160.5 24.1 %copy-start.14 = (bf16[128,16,128]{2,1,0:T(8,128)(2,1)}, bf16[128,16,128]{2,1,0:T(8,128)(2,1)S(1)}, u32[]{:S(2)}) copy-start(bf16[128,16,128]{2,1,0:T(8,128)(2,1)S(1)} %collective-permute-done.16.refs_3_) | copy-start | bytes 1572868
  172.6 12.0 %copy-start.15 = (bf16[128,16,128]{2,1,0:T(8,128)(2,1)}, bf16[128,16,128]{2,1,0:T(8,128)(2,1)S(1)}, u32[]{:S(2)}) copy-start(bf16[128,16,128]{2,1,0:T(8,128)(2,1)S(1)} %collective-permute-done.17.refs_4_) | copy-start | bytes 1572868
  184.1 0.8 copy-start.16
  184.1 1.0 copy-start.17
  277.6 11.3 %collective-permute-start.21 = (f32[4,4,16,256]{3,2,1,0:T(8,128)S(1)}, f32[4,4,16,256]{3,2,1,0:T(8,128)S(1)}, u32[]{:S(2)}, u32[]{:S(2)}) collective-permute-start(f32[4,4,16,256]{3,2,1,0:T(8,128)S(1)} %dynamic-slice_bitcast_fusion), channel_id=1, source_target_pairs={{0,4},{4,0},{1,5},{5,1},{2,6},{6,2},{3,7},{7,3},{8,12},{12,8},{9,1... | collective-permute-start | bytes 786440 | tf_op jit(solution)/shard_map/ppermute | solution.py:161
Sparse Core Ops, SparseCore 0:
  126.6 67.3 reduce-scatter.2
  197.9 78.4 reduce-scatter.4
